TPU v7x, 32 devices: a whole 2x2x4 slice. The times are simulated.
32 devices in a mesh: grp: 2 (over y), seq: 8 (over z, x), head: 2 (over core).
Axes of the slice: x: 2, y: 2, z: 4, core: 2. Of those that a mesh axis runs over, the one named last changes fastest.
Arguments:
- key_cache: bfloat16 [4, 64, 128, 1024], P('grp', ('seq', 'head')), parts along dimension 0, may hold values from -160 to 160, as said below
- value_cache: bfloat16 [4, 64, 128, 1024], P('grp', ('seq', 'head')), parts along dimension 0, may hold values from -16 to 16, as said below
- query: bfloat16 [4, 4096], P('grp', 'head'), parts along dimension 0, may hold values from -48 to 48, as said below
- lengths: int32 [4], P('grp'), parts along dimension 0, may hold values from 128 to 8192, as said below
- block_map: int32 [4, 64], P('grp'), parts along dimension 0, may hold values from 0 to 63, each once within a row
Outputs:
- attended: bfloat16 [4, 4096], P('grp', 'head'), parts along dimension 0
There are 2 independent parts, one for each index of `grp`. A program takes and returns all parts, laid end to end along the dimension named above; each array names one. Nothing has to cross between parts.
Inputs may be any that keep to these rules, and one draw needn't show every extreme that they name: `lengths`: every length is a multiple of 128; in every draw some request has length 8192. `key_cache`: finite entries, drawn afresh for every request, block, token and channel. `value_cache`: finite entries, drawn afresh for every request, block, token and channel. `query`: finite entries, drawn afresh for every request, head and channel.
All inputs are finite; a program needn't handle non-finite values.
Results may differ from a plain program's by a relative error of at most 0.0055.
Values may be sent and summed in bfloat16 or wider, within the bound.
A program may use at most 64 MiB of HBM per device.

v0:
```python
import jax
import jax.numpy as jnp
from jax import lax
from jax.sharding import PartitionSpec as P

QH = 32
KVH = 8
HD = 128
BLK = 128


def rescaled(local, top_all):
    factor = jnp.exp(local[0] - top_all)
    return (local[1] * factor, local[2] * factor[..., None])


def partials(key_rows, value_rows, queries, live_blocks):
    batch_rows = key_rows.shape[0]
    slot_count = key_rows.shape[1]
    group_count = key_rows.shape[3] // HD
    token_count = slot_count * BLK
    key_flat = key_rows.reshape(batch_rows, token_count, group_count, HD)
    value_flat = value_rows.reshape(batch_rows, token_count, group_count, HD)
    query_heads = queries.reshape(batch_rows, group_count, QH // KVH, HD)
    logit_scores = jnp.einsum(
        "bgqd,btgd->bgqt", query_heads, key_flat, preferred_element_type=jnp.float32
    )
    logit_scores = logit_scores * (1.0 / HD**0.5)
    logit_scores = logit_scores.reshape(batch_rows, group_count, QH // KVH, slot_count, BLK)
    live_mask = live_blocks[:, None, None, :, None]
    row_top = jnp.max(jnp.where(live_mask, logit_scores, jnp.float32(-1e30)), axis=(3, 4))
    expo = jnp.where(live_mask, jnp.exp(logit_scores - row_top[..., None, None]), jnp.float32(0.0))
    total = jnp.sum(expo, axis=(3, 4))
    weights = expo.astype(jnp.bfloat16).reshape(batch_rows, group_count, QH // KVH, token_count)
    summed_values = jnp.einsum(
        "bgqt,btgd->bgqd", weights, value_flat, preferred_element_type=jnp.float32
    )
    return (row_top, total, summed_values)


def owned_live(block_map, lengths, position, count):
    owned_blocks = lax.dynamic_slice_in_dim(block_map, position * count, count, 1)
    return owned_blocks < (lengths // BLK)[:, None]


def on_device(key_cache, value_cache, query, lengths, block_map):
    batch_rows = key_cache.shape[0]
    width_here = query.shape[1]
    key_rows, value_rows = (
        lax.all_to_all(key_cache, "head", split_axis=3, concat_axis=1, tiled=True),
        lax.all_to_all(value_cache, "head", split_axis=3, concat_axis=1, tiled=True),
    )
    live_blocks = owned_live(block_map, lengths, lax.axis_index("seq"), key_rows.shape[1])
    local = partials(key_rows, value_rows, query, live_blocks)
    top_every = lax.pmax(local[0], "seq")
    total, summed_values = lax.psum(rescaled(local, top_every), "seq")
    result = summed_values / total[..., None]
    return result.reshape(batch_rows, width_here).astype(jnp.bfloat16)


def solution(mesh):
    placed = (
        P("grp", ("seq", "head"), None, None),
        P("grp", ("seq", "head"), None, None),
        P("grp", "head"),
        P("grp"),
        P("grp", None),
    )
    return jax.shard_map(
        on_device, mesh=mesh, in_specs=placed, out_specs=P("grp", "head"), check_vma=False
    )
```

profile of v0, /device:TPU:0, one launch (start us, length us, event | category | flops | bytes accessed | tf_op | source)
XLA Modules:
  0.0 88.1 jit_solution(8158900298736535543)
XLA Ops:
  0.0 4.3 %copy.10 = bf16[2,4,128,1024]{2,1,0,3:T(4,128)(2,1)} copy(bf16[2,4,128,1024]{3,2,1,0:T(8,128)(2,1)} %param.5) | data formatting | bytes 4194304 | tf_op args[0]
  4.3 0.0 copy-start.2
  4.3 0.0 copy-start.1
  4.3 0.0 copy-start
  4.3 3.9 %all-to-all-start = ((bf16[2,4,128,1024]{2,1,0,3:T(4,128)(2,1)}), bf16[2,4,128,1024]{2,1,0,3:T(4,128)(2,1)S(1)}, u32[]{:S(2)}, u32[]{:S(2)}) async-start(bf16[2,4,128,1024]{2,1,0,3:T(4,128)(2,1)} %copy.10), calls=%async_computation | async-start | bytes 4194304 | tf_op jit(solution)/shard_map/all_to_all | solution.py:50
  8.2 0.0 copy-done.2
  8.3 0.0 copy-done.1
  8.3 0.1 dynamic-slice_compare_fusion
  8.3 0.1 broadcast_bitcast_fusion
  8.4 0.0 copy-done
  8.5 4.3 %copy.13 = bf16[2,4,128,1024]{2,1,0,3:T(4,128)(2,1)} copy(bf16[2,4,128,1024]{3,2,1,0:T(8,128)(2,1)} %param.6) | data formatting | bytes 4194304 | tf_op args[1]
  12.8 0.0 all-to-all-done
  12.8 4.8 %all-to-all-start.1 = ((bf16[2,4,128,1024]{2,1,0,3:T(4,128)(2,1)}), bf16[2,4,128,1024]{2,1,0,3:T(4,128)(2,1)}, u32[]{:S(2)}, u32[]{:S(2)}) async-start(bf16[2,4,128,1024]{2,1,0,3:T(4,128)(2,1)} %copy.13), calls=%async_computation.1 | async-start | bytes 4194304 | tf_op jit(solution)/shard_map/all_to_all | solution.py:51
  17.6 3.0 %copy.11 = bf16[2,4,128,2,512]{4,2,1,3,0:T(8,128)(2,1)} copy(bf16[2,4,128,2,512]{2,1,0,4,3:T(4,128)(2,1)S(1)} %bitcast.19) | data formatting | bytes 4194304 | tf_op jit(solution)/shard_map/all_to_all | solution.py:50
  20.6 2.5 %reshape.24 = bf16[2,1024,4,128]{3,2,1,0:T(4,128)(2,1)S(1)} reshape(bf16[2,2,4,128,512]{4,3,2,1,0:T(8,128)(2,1)} %bitcast.20) | data formatting | bytes 4194304 | tf_op jit(solution)/shard_map/reshape | solution.py:22
  23.2 0.7 select_reduce_fusion
  23.9 23.1 %pmax.7 = f32[2,4,4]{2,1,0:T(4,128)S(1)} all-reduce(f32[2,4,4]{2,1,0:T(4,128)S(1)} %get-tuple-element.9), channel_id=1, replica_groups=mesh['grp'=2,'seq'=8,'head'=2] {'seq'}, use_global_device_ids=true, to_apply=%region_1.2 | all-reduce | flops 32 | bytes 256 | tf_op jit(solution)/shard_map/pmax | solution.py:55
  47.0 0.2 fusion.10
  47.3 0.0 all-to-all-done.1
  47.3 3.0 %copy.14 = bf16[2,4,128,2,512]{4,2,1,3,0:T(8,128)(2,1)S(1)} copy(bf16[2,4,128,2,512]{2,1,0,4,3:T(4,128)(2,1)} %bitcast.2) | data formatting | bytes 4194304 | tf_op jit(solution)/shard_map/all_to_all | solution.py:51
  50.2 2.1 %reshape.25 = bf16[2,1024,4,128]{3,2,1,0:T(4,128)(2,1)} reshape(bf16[2,2,4,128,512]{4,3,2,1,0:T(8,128)(2,1)S(1)} %bitcast.21) | data formatting | bytes 4194304 | tf_op jit(solution)/shard_map/reshape | solution.py:23
  52.3 2.0 %fusion.7 = f32[2,4,4,128]{3,2,1,0:T(4,128)S(1)} fusion(bf16[2,1024,4,128]{3,2,1,0:T(4,128)(2,1)} %reshape.25, f32[2,4,4,1024]{3,2,1,0:T(4,128)S(1)} %get-tuple-element.10, f32[2,4,4]{2,1,0:T(4,128)S(1)} %get-tuple-element.9, pred[2,1024]{1,0:T(4,128)(4,1)S(1)} %bitcast.27, f32[2,4,4]{2,1,0:T(4,128)S(1)} %bitcast.29), kind=kOutput, calls=%fused_computation.5 | convolution fusion | flops 8491008 | bytes 2246912 | tf_op jit(solution)/shard_map/bgqt,btgd->bgqd/dot_general | solution.py:35
  54.4 33.0 %all-reduce = (f32[2,4,4,128]{3,2,1,0:T(4,128)S(1)}, f32[2,4,4]{2,1,0:T(4,128)S(1)}) all-reduce(f32[2,4,4,128]{3,2,1,0:T(4,128)S(1)} %fusion.7, f32[2,4,4]{2,1,0:T(4,128)S(1)} %bitcast.24), channel_id=1, replica_groups=mesh['grp'=2,'seq'=8,'head'=2] {'seq'}, use_global_device_ids=true, to_apply=%region_2.3 | all-reduce | flops 4128 | bytes 33024 | tf_op jit(solution)/shard_map/psum | solution.py:56
  87.4 0.1 divide_convert_fusion
  87.5 0.6 convert_element_type.12
  (4 shorter events, 0.0 us)
Async XLA Ops:
  4.3 3.9 %copy-start.2 = (s32[2]{0:T(128)S(1)}, s32[2]{0:T(128)}, u32[]{:S(2)}) copy-start(s32[2]{0:T(128)} %param.8) | copy-start | bytes 28
  4.3 3.9 %copy-start.1 = (s32[2,64]{1,0:T(2,128)S(1)}, s32[2,64]{1,0:T(2,128)}, u32[]{:S(2)}) copy-start(s32[2,64]{1,0:T(2,128)} %param.9) | copy-start | bytes 1540
  4.3 4.1 %copy-start = (bf16[2,2048]{1,0:T(2,128)(2,1)S(1)}, bf16[2,2048]{1,0:T(2,128)(2,1)}, u32[]{:S(2)}) copy-start(bf16[2,2048]{1,0:T(2,128)(2,1)} %param.7) | copy-start | bytes 24580
  4.3 8.5 %all-to-all-start = ((bf16[2,4,128,1024]{2,1,0,3:T(4,128)(2,1)}), bf16[2,4,128,1024]{2,1,0,3:T(4,128)(2,1)S(1)}, u32[]{:S(2)}, u32[]{:S(2)}) async-start(bf16[2,4,128,1024]{2,1,0,3:T(4,128)(2,1)} %copy.10), calls=%async_computation | async-start | bytes 4194304 | tf_op jit(solution)/shard_map/all_to_all | solution.py:50
  12.8 34.5 %all-to-all-start.1 = ((bf16[2,4,128,1024]{2,1,0,3:T(4,128)(2,1)}), bf16[2,4,128,1024]{2,1,0,3:T(4,128)(2,1)}, u32[]{:S(2)}, u32[]{:S(2)}) async-start(bf16[2,4,128,1024]{2,1,0,3:T(4,128)(2,1)} %copy.13), calls=%async_computation.1 | async-start | bytes 4194304 | tf_op jit(solution)/shard_map/all_to_all | solution.py:51
where the time goes:
time: 88.7 us; the launch traced here: 88.1 us
  blocking collectives  56.2 us (63%)
  local copies, waits for them, and re-layouts  20 us (23%)
  starting transfers between devices  8.72 us (10%)
  matrix products  2.79 us (3%)
    psum x1, blocking collectives, on_device(): total, summed_values = lax.psum(rescaled(local, top_every), 'seq')  33 us
    pmax x1, blocking collectives, on_device(): top_every = lax.pmax(local[0], 'seq')  23.1 us
    unnamed x10, local copies, waits for them, and re-layouts  8.71 us
    all_to_all x1, starting transfers between devices, on_device(): lax.all_to_all(value_cache, 'head', split_axis=3, concat_axis=1, tiled=True)  4.82 us
    all_to_all x1, starting transfers between devices, on_device(): lax.all_to_all(key_cache, 'head', split_axis=3, concat_axis=1, tiled=True)  3.9 us
    all_to_all x1, local copies, waits for them, and re-layouts, on_device(): lax.all_to_all(key_cache, 'head', split_axis=3, concat_axis=1, tiled=True)  3.04 us
    all_to_all x1, local copies, waits for them, and re-layouts, on_device(): lax.all_to_all(value_cache, 'head', split_axis=3, concat_axis=1, tiled=True)  2.97 us
    reshape x1, local copies, waits for them, and re-layouts, partials(): key_flat = key_rows.reshape(batch_rows, token_count, group_count, HD)  2.55 us
  transfers between devices with their start and end apart: 2, of which 0 were waited for; matrix products, arithmetic and copies ran while one was open for 13% of the time, Pallas kernels for 0%

commit v1 on v0

--- a/solution.py
+++ b/solution.py
@@ -47,7 +47,12 @@
     batch_rows = key_cache.shape[0]
     width_here = query.shape[1]
     key_rows, value_rows = (
-        lax.all_to_all(key_cache, "head", split_axis=3, concat_axis=1, tiled=True),
+        jnp.concatenate(
+            lax.all_to_all(
+                jnp.stack(jnp.split(key_cache, lax.axis_size("head"), axis=3)), "head", 0, 0
+            ),
+            axis=1,
+        ),
         lax.all_to_all(value_cache, "head", split_axis=3, concat_axis=1, tiled=True),
     )
     live_blocks = owned_live(block_map, lengths, lax.axis_index("seq"), key_rows.shape[1])

time: 88.7 us -> 86.1 us (0.971)
  local copies, waits for them, and re-layouts: 20 us -> 15.9 us
  other arithmetic: 0.39 us -> 1.86 us
    unnamed x10 -> x9, local copies, waits for them, and re-layouts: 8.71 us -> 4.4 us
    another operation x0 -> x2, local copies, waits for them, and re-layouts: none -> 4.3 us  [the longest x1 2.56 us: partials(): key_flat = key_rows.reshape(batch_rows, token_count, group_count, HD)]
    all_to_all x1 -> x0, local copies, waits for them, and re-layouts: 3.04 us -> none  [on_device(): lax.all_to_all(key_cache, 'head', split_axis=3, concat_axis=1, tiled=True)]
    another operation x0 -> x1, other arithmetic: none -> 1.48 us  [on_device(): jnp.stack(jnp.split(key_cache, lax.axis_size('head'), axis=3))]
    reshape x1, local copies, waits for them, and re-layouts: 2.55 us -> 1.54 us  [on_device(): jnp.concatenate(lax.all_to_all(jnp.stack(jnp.split(key_cache, lax.axis_si...]
  transfers between devices with their start and end apart: 2 -> 2, of which waited for: 0 -> 0; matrix products, arithmetic and copies ran while one was open for 13% -> 11% of each run, Pallas kernels for 0% -> 0%
where the time goes in v1:
time: 86.1 us; the launch traced here: 85.5 us
  blocking collectives  56.2 us (65%)
  local copies, waits for them, and re-layouts  15.9 us (18%)
  starting transfers between devices  8.71 us (10%)
  matrix products  2.79 us (3%)
  other arithmetic  1.86 us (2%)
    psum x1, blocking collectives, on_device(): total, summed_values = lax.psum(rescaled(local, top_every), 'seq')  33 us
    pmax x1, blocking collectives, on_device(): top_every = lax.pmax(local[0], 'seq')  23.1 us
    all_to_all x1, starting transfers between devices, on_device(): lax.all_to_all(value_cache, 'head', split_axis=3, concat_axis=1, tiled=True)  4.82 us
    unnamed x9, local copies, waits for them, and re-layouts  4.4 us
    all_to_all x1, starting transfers between devices, on_device(): lax.all_to_all(jnp.stack(jnp.split(key_cache, lax.axis_size('head'), axis...  3.89 us
    all_to_all x1, local copies, waits for them, and re-layouts, on_device(): lax.all_to_all(value_cache, 'head', split_axis=3, concat_axis=1, tiled=True)  2.97 us
    another operation x1, local copies, waits for them, and re-layouts, partials(): key_flat = key_rows.reshape(batch_rows, token_count, group_count, HD)  2.56 us
    reshape x1, local copies, waits for them, and re-layouts, partials(): value_flat = value_rows.reshape(batch_rows, token_count, group_count, HD)  2.09 us
  transfers between devices with their start and end apart: 2, of which 0 were waited for; matrix products, arithmetic and copies ran while one was open for 11% of the time, Pallas kernels for 0%

profile of v1, /device:TPU:0, one launch (start us, length us, event | category | flops | bytes accessed | tf_op | source)
XLA Modules:
  0.0 85.5 jit_solution(14250481112158091273)
XLA Ops:
  0.0 1.7 %slice_bitcast_fusion.1 = (bf16[1,2,4,128,512]{4,3,2,1,0:T(8,128)(2,1)S(1)}, bf16[1,2,4,128,512]{4,3,2,1,0:T(8,128)(2,1)S(1)}) fusion(bf16[2,4,128,1024]{3,2,1,0:T(8,128)(2,1)} %param.5), kind=kLoop, calls=%fused_computation.8 | loop fusion | bytes 4194304 | tf_op jit(solution)/shard_map/stack | solution.py:52
  1.7 1.5 %pad_maximum_fusion = bf16[2,2,4,128,512]{4,3,2,1,0:T(8,128)(2,1)} fusion(bf16[1,2,4,128,512]{4,3,2,1,0:T(8,128)(2,1)S(1)} %get-tuple-element.10, bf16[1,2,4,128,512]{4,3,2,1,0:T(8,128)(2,1)S(1)} %get-tuple-element.9), kind=kLoop, calls=%fused_computation | loop fusion | flops 1048576 | bytes 4194304 | tf_op jit(solution)/shard_map/stack | solution.py:52
  3.2 0.0 copy-start.2
  3.2 0.0 copy-start.1
  3.2 3.9 %all-to-all-start = ((bf16[2,2,4,128,512]{4,3,2,1,0:T(8,128)(2,1)}), bf16[2,2,4,128,512]{4,3,2,1,0:T(8,128)(2,1)S(1)}, u32[]{:S(2)}, u32[]{:S(2)}) async-start(bf16[2,2,4,128,512]{4,3,2,1,0:T(8,128)(2,1)} %pad_maximum_fusion), calls=%async_computation | async-start | bytes 4194304 | tf_op jit(solution)/shard_map/all_to_all | solution.py:51
  7.1 0.0 copy-done.2
  7.2 0.0 copy-done.1
  7.2 0.1 dynamic-slice_compare_fusion
  7.3 0.1 broadcast_bitcast_fusion
  7.3 4.3 %copy.12 = bf16[2,4,128,1024]{2,1,0,3:T(4,128)(2,1)} copy(bf16[2,4,128,1024]{3,2,1,0:T(8,128)(2,1)} %param.6) | data formatting | bytes 4194304 | tf_op args[1]
  11.6 0.0 all-to-all-done
  11.6 4.8 %all-to-all-start.1 = ((bf16[2,4,128,1024]{2,1,0,3:T(4,128)(2,1)}), bf16[2,4,128,1024]{2,1,0,3:T(4,128)(2,1)}, u32[]{:S(2)}, u32[]{:S(2)}) async-start(bf16[2,4,128,1024]{2,1,0,3:T(4,128)(2,1)} %copy.12), calls=%async_computation.1 | async-start | bytes 4194304 | tf_op jit(solution)/shard_map/all_to_all | solution.py:56
  16.5 1.5 %copy.10 = bf16[2,2,4,128,512]{4,3,2,1,0:T(8,128)(2,1)} copy(bf16[2,2,4,128,512]{4,3,2,0,1:T(8,128)(2,1)S(1)} %bitcast.26) | data formatting | bytes 4194304 | tf_op jit(solution)/shard_map/reshape | solution.py:50
  18.0 0.0 copy-start
  18.0 2.6 %reshape_reshape.3 = bf16[2,1024,4,128]{3,2,1,0:T(4,128)(2,1)S(1)} reshape(bf16[2,2,4,128,512]{4,3,2,1,0:T(8,128)(2,1)} %copy.10) | data formatting | bytes 4194304 | tf_op jit(solution)/shard_map/reshape;reshape | solution.py:22
  20.6 0.0 copy-done
  20.6 0.7 select_reduce_fusion
  21.3 23.1 %pmax.7 = f32[2,4,4]{2,1,0:T(4,128)S(1)} all-reduce(f32[2,4,4]{2,1,0:T(4,128)S(1)} %get-tuple-element.11), channel_id=1, replica_groups=mesh['grp'=2,'seq'=8,'head'=2] {'seq'}, use_global_device_ids=true, to_apply=%region_1.2 | all-reduce | flops 32 | bytes 256 | tf_op jit(solution)/shard_map/pmax | solution.py:60
  44.5 0.2 bitcast_reduce_fusion
  44.7 0.0 all-to-all-done.1
  44.7 3.0 %copy.13 = bf16[2,4,128,2,512]{4,2,1,3,0:T(8,128)(2,1)S(1)} copy(bf16[2,4,128,2,512]{2,1,0,4,3:T(4,128)(2,1)} %bitcast.4) | data formatting | bytes 4194304 | tf_op jit(solution)/shard_map/all_to_all | solution.py:56
  47.7 2.1 %reshape.24 = bf16[2,1024,4,128]{3,2,1,0:T(4,128)(2,1)} reshape(bf16[2,2,4,128,512]{4,3,2,1,0:T(8,128)(2,1)S(1)} %bitcast.27) | data formatting | bytes 4194304 | tf_op jit(solution)/shard_map/reshape | solution.py:23
  49.8 2.0 %fusion.7 = f32[2,4,4,128]{3,2,1,0:T(4,128)S(1)} fusion(bf16[2,1024,4,128]{3,2,1,0:T(4,128)(2,1)} %reshape.24, f32[2,4,1024,4]{2,3,1,0:T(4,128)S(1)} %get-tuple-element.12, f32[2,4,4]{2,1,0:T(4,128)S(1)} %get-tuple-element.11, pred[2,1024]{1,0:T(4,128)(4,1)S(1)} %bitcast.33, f32[2,4,4]{2,1,0:T(4,128)S(1)} %bitcast.35), kind=kOutput, calls=%fused_computation.6 | convolution fusion | flops 8491008 | bytes 2246912 | tf_op jit(solution)/shard_map/bgqt,btgd->bgqd/dot_general | solution.py:35
  51.8 33.0 %all-reduce = (f32[2,4,4,128]{3,2,1,0:T(4,128)S(1)}, f32[2,4,4]{2,1,0:T(4,128)S(1)}) all-reduce(f32[2,4,4,128]{3,2,1,0:T(4,128)S(1)} %fusion.7, f32[2,4,4]{2,1,0:T(4,128)S(1)} %bitcast.30), channel_id=1, replica_groups=mesh['grp'=2,'seq'=8,'head'=2] {'seq'}, use_global_device_ids=true, to_apply=%region_2.3 | all-reduce | flops 4128 | bytes 33024 | tf_op jit(solution)/shard_map/psum | solution.py:61
  84.8 0.1 divide_convert_fusion
  84.9 0.6 convert_element_type.12
  (4 shorter events, 0.0 us)
Async XLA Ops:
  3.2 3.9 %copy-start.2 = (s32[2]{0:T(128)S(1)}, s32[2]{0:T(128)}, u32[]{:S(2)}) copy-start(s32[2]{0:T(128)} %param.8) | copy-start | bytes 28
  3.2 3.9 %copy-start.1 = (s32[2,64]{1,0:T(2,128)S(1)}, s32[2,64]{1,0:T(2,128)}, u32[]{:S(2)}) copy-start(s32[2,64]{1,0:T(2,128)} %param.9) | copy-start | bytes 1540
  3.2 8.4 %all-to-all-start = ((bf16[2,2,4,128,512]{4,3,2,1,0:T(8,128)(2,1)}), bf16[2,2,4,128,512]{4,3,2,1,0:T(8,128)(2,1)S(1)}, u32[]{:S(2)}, u32[]{:S(2)}) async-start(bf16[2,2,4,128,512]{4,3,2,1,0:T(8,128)(2,1)} %pad_maximum_fusion), calls=%async_computation | async-start | bytes 4194304 | tf_op jit(solution)/shard_map/all_to_all | solution.py:51
  11.6 33.0 %all-to-all-start.1 = ((bf16[2,4,128,1024]{2,1,0,3:T(4,128)(2,1)}), bf16[2,4,128,1024]{2,1,0,3:T(4,128)(2,1)}, u32[]{:S(2)}, u32[]{:S(2)}) async-start(bf16[2,4,128,1024]{2,1,0,3:T(4,128)(2,1)} %copy.12), calls=%async_computation.1 | async-start | bytes 4194304 | tf_op jit(solution)/shard_map/all_to_all | solution.py:56
  18.0 2.6 %copy-start = (bf16[2,2048]{1,0:T(2,128)(2,1)S(1)}, bf16[2,2048]{1,0:T(2,128)(2,1)}, u32[]{:S(2)}) copy-start(bf16[2,2048]{1,0:T(2,128)(2,1)} %param.7) | copy-start | bytes 24580
